TPU v7x, 32 devices: a whole 2x2x4 slice. The times are simulated.
32 devices in a mesh: tm: 8 (over z, x), env: 4 (over y, core).
Axes of the slice: x: 2, y: 2, z: 4, core: 2. Of those that a mesh axis runs over, the one named last changes fastest.
Arguments:
- init_state: float32 [70, 1024], P(None, 'env'), may hold values from -6 to 6
- torque: float32 [32, 35, 1024], P('tm', None, 'env'), may hold values from -192 to 192
- contact: int32 [32, 1024], P('tm', 'env'), may hold values 0 or 1
- mass_inverse: float32 [16, 35, 35], P('tm'), may hold values from -0.014 to 1.5, as said below
- stiffness: float32 [35], replicated, may hold values from 10 to 100
- damping: float32 [35], replicated, may hold values from 0.5 to 5
- gravity: float32 [35], replicated, may hold values from 1 to 10
- contact_stiffness: float32 [35], replicated, may hold values from 20 to 100
- contact_damping: float32 [35], replicated, may hold values from 0.5 to 3
Outputs:
- final_states: float32 [16, 70, 1024], P('tm', None, 'env')
- corrections: float32 [3, 1024], P(None, 'env')
Inputs may be any that keep to these rules, and one draw needn't show every extreme that they name: `mass_inverse`: each matrix is symmetric, and each diagonal entry exceeds the sum of the magnitudes of the other entries of its row.
All inputs are finite; a program needn't handle non-finite values. No bound on the sum of `contact` on one device may be relied on, other than what follows from the above.
Results may differ from a plain program's by a relative error of at most 0.00025.
Values sent between devices are 32-bit elements; how exact they have to be, the bound alone decides.
A program may use at most 64 MiB of HBM per device.

v0:
```python
import jax
import jax.numpy as jnp
from jax import lax
from jax.sharding import PartitionSpec as P

DOF = 35
HS = 2
SUB = 32
ITERS = 3
step_length = 0.05


def exact_dot(left, right):
    return jnp.dot(left, right, precision=lax.Precision.HIGHEST, preferred_element_type=jnp.float32)


def coarse_one(state_now, torque_steps, mean_steps, inverse, params):
    stiffness, damping, gravity, contact_stiffness, contact_damping = params
    joint_pos = state_now[:DOF]
    joint_vel = state_now[DOF:]
    for step_pos in range(HS):
        spring = (stiffness + gravity + mean_steps[step_pos] * contact_stiffness)[:, None]
        friction = (damping + mean_steps[step_pos] * contact_damping)[:, None]
        force = torque_steps[step_pos] - spring * joint_pos - friction * joint_vel
        joint_vel = joint_vel + step_length * exact_dot(inverse, force)
        joint_pos = joint_pos + step_length * joint_vel
    return jnp.concatenate([joint_pos, joint_vel], axis=0)


def fine_one(state_now, torque_steps, contact_steps, inverse, params):
    stiffness, damping, gravity, contact_stiffness, contact_damping = params
    fine_dt = step_length / SUB
    joint_pair = (state_now[:DOF], state_now[DOF:])
    for step_pos in range(HS):
        torque_here = torque_steps[step_pos]
        contact_here = contact_steps[step_pos][None, :]

        def substep(counter, pair_now):
            joint_pos, joint_vel = pair_now
            force = (
                torque_here
                - stiffness[:, None] * joint_pos
                - damping[:, None] * joint_vel
                - gravity[:, None] * jnp.sin(joint_pos)
                - contact_here
                * (contact_stiffness[:, None] * joint_pos + contact_damping[:, None] * joint_vel)
            )
            joint_vel = joint_vel + fine_dt * exact_dot(inverse, force)
            joint_pos = joint_pos + fine_dt * joint_vel
            return (joint_pos, joint_vel)

        joint_pair = lax.fori_loop(0, SUB, substep, joint_pair, unroll=min(8, SUB))
    return jnp.concatenate([joint_pair[0], joint_pair[1]], axis=0)


def body(
    init_state,
    torque,
    contact,
    mass_inverse,
    stiffness,
    damping,
    gravity,
    contact_stiffness,
    contact_damping,
):
    params = (stiffness, damping, gravity, contact_stiffness, contact_damping)
    local_slices = mass_inverse.shape[0]
    env_local = init_state.shape[1]
    state_rows = init_state.shape[0]
    torque_steps = torque.reshape(local_slices, HS, DOF, env_local)
    contact_float = contact.astype(jnp.float32)
    contact_steps = contact_float.reshape(local_slices, HS, env_local)
    totals = lax.psum(jnp.sum(contact_float, axis=1), "env")
    mean_steps = (totals / (env_local * lax.axis_size("env"))).reshape(local_slices, HS)
    eye_state = jnp.eye(state_rows, dtype=jnp.float32)
    zero_shift = jnp.zeros((state_rows, env_local), jnp.float32)
    no_force = jnp.zeros((local_slices, HS, DOF, 1), jnp.float32)
    step_maps = jax.vmap(coarse_one, in_axes=(None, 0, 0, 0, None))(
        eye_state, no_force, mean_steps, mass_inverse, params
    )
    coarse_free = jax.vmap(coarse_one, in_axes=(0, 0, 0, 0, None))(
        jnp.zeros((local_slices, state_rows, env_local), jnp.float32),
        torque_steps,
        mean_steps,
        mass_inverse,
        params,
    )
    device_map = eye_state
    for slot_pos in range(local_slices):
        device_map = exact_dot(step_maps[slot_pos], device_map)
    all_maps = lax.all_gather(device_map[None], "tm", axis=0, tiled=True)
    my_index = lax.axis_index("tm")

    def backward(product, inputs):
        position, this_map = inputs
        active = position < my_index
        emitted = jnp.where(active, product, 0.0)
        following = jnp.where(active, exact_dot(product, this_map), eye_state)
        return (following, emitted)

    positions = jnp.arange(lax.axis_size("tm"), dtype=jnp.int32)
    lead_map, phi_rows = lax.scan(backward, eye_state, (positions, all_maps), reverse=True)
    lead_state = exact_dot(lead_map, init_state)

    def sweep(offsets):
        local_shift = zero_shift
        for slot_pos in range(local_slices):
            local_shift = exact_dot(step_maps[slot_pos], local_shift) + offsets[slot_pos]
        entry = lead_state + jnp.einsum(
            "mij,mje->ie",
            phi_rows,
            lax.all_gather(local_shift[None], "tm", axis=0, tiled=True),
            precision=lax.Precision.HIGHEST,
        )
        start_list = []
        end_list = []
        current = entry
        for slot_pos in range(local_slices):
            start_list.append(current)
            current = exact_dot(step_maps[slot_pos], current) + offsets[slot_pos]
            end_list.append(current)
        return (jnp.stack(start_list), jnp.stack(end_list))

    starts, ends = sweep(coarse_free)
    fine_all = jax.vmap(fine_one, in_axes=(0, 0, 0, 0, None))
    records = []
    for iteration in range(ITERS):
        fine_end = fine_all(starts, torque_steps, contact_steps, mass_inverse, params)
        jumps = fine_end - jnp.einsum(
            "sij,sje->sie", step_maps, starts, precision=lax.Precision.HIGHEST
        )
        new_starts, new_ends = sweep(jumps)
        local_max = jnp.max(jnp.sqrt(jnp.sum((new_ends - ends) ** 2, axis=1)), axis=0)
        records.append(lax.pmax(local_max, "tm"))
        starts, ends = (new_starts, new_ends)
    corrections = jnp.stack(records)
    return (ends, corrections)


def solution(mesh):
    placed = (
        P(None, "env"),
        P("tm", None, "env"),
        P("tm", "env"),
        P("tm", None, None),
        P(),
        P(),
        P(),
        P(),
        P(),
    )
    return jax.shard_map(
        body,
        mesh=mesh,
        in_specs=placed,
        out_specs=(P("tm", None, "env"), P(None, "env")),
        check_vma=False,
    )
```

profile of v0, /device:TPU:0, one launch (start us, length us, event | category | flops | bytes accessed | tf_op | source)
XLA Modules:
  0.0 318.0 jit_solution(16330962543061578949)
XLA Ops:
  0.6 0.8 convert_reduce_fusion
  1.5 8.4 %psum.7 = f32[4]{0:T(128)S(1)} all-reduce(f32[4]{0:T(128)S(1)} %convert_reduce_fusion), channel_id=1, replica_groups=mesh['tm'=8,'env'=4] {'env'}, use_global_device_ids=true, to_apply=%region_1.0 | all-reduce | flops 4 | bytes 32 | tf_op jit(solution)/shard_map/psum | solution.py:74
  10.2 0.6 copy-done.4
  10.8 0.6 copy-done.1
  11.8 0.7 copy-done.6
  13.6 31.3 %all-gather.5 = f32[8,70,70]{2,1,0:T(8,128)S(1)} all-gather(f32[1,70,70]{2,1,0:T(8,128)S(1)} %convolution_bitcast_fusion.5), channel_id=2, replica_groups=mesh['tm'=8,'env'=4] {'tm'}, dimensions={0}, use_global_device_ids=true | all-gather | bytes 176400 | tf_op jit(solution)/shard_map/all_gather | solution.py:92
  44.9 12.7 %while.95 = (s32[]{:T(128)}, f32[70,70]{0,1:T(8,128)S(1)}, f32[8,70,70]{1,2,0:T(8,128)S(1)}, s32[8]{0:T(128)S(1)}, s32[]{:T(128)}, /*index=5*/f32[8,70,70]{2,1,0:T(8,128)S(1)}, s32[]{:T(128)}, s32[]{:T(128)}) while((s32[]{:T(128)}, f32[70,70]{0,1:T(8,128)S(1)}, f32[8,70,70]{1,2,0:T(8,128)S(1)}, s32[8]{0:T(128)S(1)}, s32[]{:T(128)}, ...), condition=%wide.region_3.4_spmd.clone, body=%wide.region_2.3_spmd.clone.sunk | while | flops 4135604 | bytes 206392 | solution.py:103
  59.6 31.5 %all-gather.6 = f32[8,70,256]{2,1,0:T(8,128)S(1)} all-gather(f32[1,70,256]{2,1,0:T(8,128)S(1)} %fusion.1027), channel_id=3, replica_groups=mesh['tm'=8,'env'=4] {'tm'}, dimensions={0}, use_global_device_ids=true | all-gather | bytes 645120 | tf_op jit(solution)/shard_map/all_gather | solution.py:113
  91.1 0.7 fusion.1026
  92.3 0.7 copy-done.8
  93.1 17.1 %while.89 = (s32[]{:T(128)}, f32[2,35,256]{2,1,0:T(8,128)S(1)}, f32[2,35,256]{2,1,0:T(8,128)S(1)}, f32[35]{0:T(128)S(1)}, f32[2,35,256]{2,1,0:T(8,128)S(1)}, /*i...) while((s32[]{:T(128)}, f32[2,35,256]{2,1,0:T(8,128)S(1)}, ...), condition=%wide.region_5.6_spmd, body=%wide.region_4.5_spmd.sunk | while | flops 62504960 | bytes 2680981 | solution.py:52
  110.2 17.2 %while.90 = (s32[]{:T(128)}, f32[2,35,256]{2,1,0:T(8,128)S(1)}, f32[2,35,256]{2,1,0:T(8,128)S(1)}, f32[35]{0:T(128)S(1)}, f32[2,35,256]{2,1,0:T(8,128)S(1)}, /*i...) while((s32[]{:T(128)}, f32[2,35,256]{2,1,0:T(8,128)S(1)}, ...), condition=%wide.region_7.8_spmd, body=%wide.region_6.7_spmd.sunk | while | flops 62504960 | bytes 2680981 | solution.py:52
  127.9 31.5 %all-gather.7 = f32[8,70,256]{2,1,0:T(8,128)S(1)} all-gather(f32[1,70,256]{2,1,0:T(8,128)S(1)} %fusion.1025), channel_id=4, replica_groups=mesh['tm'=8,'env'=4] {'tm'}, dimensions={0}, use_global_device_ids=true | all-gather | bytes 645120 | tf_op jit(solution)/shard_map/all_gather | solution.py:113
  159.4 0.7 fusion.1024
  160.5 17.2 %while.91 = (s32[]{:T(128)}, f32[2,35,256]{2,1,0:T(8,128)S(1)}, f32[2,35,256]{2,1,0:T(8,128)S(1)}, f32[35]{0:T(128)S(1)}, f32[2,35,256]{2,1,0:T(8,128)S(1)}, /*i...) while((s32[]{:T(128)}, f32[2,35,256]{2,1,0:T(8,128)S(1)}, ...), condition=%wide.region_9.10_spmd, body=%wide.region_8.9_spmd.sunk | while | flops 62504960 | bytes 2680981 | solution.py:52
  177.7 17.2 %while.92 = (s32[]{:T(128)}, f32[2,35,256]{2,1,0:T(8,128)S(1)}, f32[2,35,256]{2,1,0:T(8,128)S(1)}, f32[35]{0:T(128)S(1)}, f32[2,35,256]{2,1,0:T(8,128)S(1)}, /*i...) while((s32[]{:T(128)}, f32[2,35,256]{2,1,0:T(8,128)S(1)}, ...), condition=%wide.region_11.12_spmd, body=%wide.region_10.11_spmd.sunk | while | flops 62504960 | bytes 2680981 | solution.py:52
  195.3 31.5 %all-gather.8 = f32[8,70,256]{2,1,0:T(8,128)S(1)} all-gather(f32[1,70,256]{2,1,0:T(8,128)S(1)} %fusion.1023), channel_id=5, replica_groups=mesh['tm'=8,'env'=4] {'tm'}, dimensions={0}, use_global_device_ids=true | all-gather | bytes 645120 | tf_op jit(solution)/shard_map/all_gather | solution.py:113
  226.9 0.7 fusion.1022
  228.0 17.2 %while.93 = (s32[]{:T(128)}, f32[2,35,256]{2,1,0:T(8,128)S(1)}, f32[2,35,256]{2,1,0:T(8,128)S(1)}, f32[35]{0:T(128)S(1)}, f32[2,35,256]{2,1,0:T(8,128)S(1)}, /*i...) while((s32[]{:T(128)}, f32[2,35,256]{2,1,0:T(8,128)S(1)}, ...), condition=%wide.region_13.14_spmd, body=%wide.region_12.13_spmd.sunk | while | flops 62504960 | bytes 2680981 | solution.py:52
  245.1 17.2 %while.94 = (s32[]{:T(128)}, f32[2,35,256]{2,1,0:T(8,128)S(1)}, f32[2,35,256]{2,1,0:T(8,128)S(1)}, f32[35]{0:T(128)S(1)}, f32[2,35,256]{2,1,0:T(8,128)S(1)}, /*i...) while((s32[]{:T(128)}, f32[2,35,256]{2,1,0:T(8,128)S(1)}, ...), condition=%wide.region_15.16_spmd, body=%wide.region_14.15_spmd.sunk | while | flops 62504960 | bytes 2680981 | solution.py:52
  262.8 31.3 %all-gather.9 = f32[8,70,256]{2,1,0:T(8,128)S(1)} all-gather(f32[1,70,256]{2,1,0:T(8,128)S(1)} %fusion.1021), channel_id=6, replica_groups=mesh['tm'=8,'env'=4] {'tm'}, dimensions={0}, use_global_device_ids=true | all-gather | bytes 645120 | tf_op jit(solution)/shard_map/all_gather | solution.py:113
  294.2 0.7 fusion.1020
  295.3 0.7 copy.115
  296.1 21.2 %all-reduce = (f32[1,256]{1,0:T(1,128)S(1)}, f32[1,256]{1,0:T(1,128)S(1)}, f32[1,256]{1,0:T(1,128)S(1)}) all-reduce(f32[1,256]{1,0:T(1,128)S(1)} %bitcast.663, f32[1,256]{1,0:T(1,128)S(1)} %bitcast.664, f32[1,256]{1,0:T(1,128)S(1)} %bitcast.662), channel_id=1, replica_groups=mesh['tm'=8,'env'=4] {'tm'}, use_global_device_ids=true, to_apply=%region_24.25 | all-reduce | flops 768 | bytes 6144 | tf_op jit(solution)/shard_map/pmax | solution.py:135
  (294 shorter events, 116.0 us)
Async XLA Ops:
  0.6 56.9 %copy-start = (f32[70,256]{1,0:T(8,128)S(1)}, f32[70,256]{1,0:T(8,128)}, u32[]{:S(2)}) copy-start(f32[70,256]{1,0:T(8,128)} %param.23) | copy-start | bytes 215044
  10.2 0.7 copy-start.4
  10.2 0.7 copy-start.5
  10.8 0.7 copy-start.1
  10.8 0.7 copy-start.2
  10.8 0.7 copy-start.3
  11.8 0.8 copy-start.6
  57.6 0.9 copy-start.7
  92.3 0.7 copy-start.8
where the time goes:
time: 318 us
  blocking collectives  187 us (59%)
  matrix products  111 us (35%)
  local copies, waits for them, and re-layouts  9.75 us (3%)
  loops' own time  7.26 us (2%)
    all_gather x4, blocking collectives, sweep(): lax.all_gather(local_shift[None], 'tm', axis=0, tiled=True)  126 us
    dot_general x220, matrix products, exact_dot(): jnp.dot(left, right, precision=lax.Precision.HIGHEST, preferred_element_t...  108 us
    all_gather x1, blocking collectives, body(): all_maps = lax.all_gather(device_map[None], 'tm', axis=0, tiled=True)  31.3 us
    pmax x1, blocking collectives, body(): records.append(lax.pmax(local_max, 'tm'))  21.2 us
    psum x1, blocking collectives, body(): totals = lax.psum(jnp.sum(contact_float, axis=1), 'env')  8.39 us

commit v1 on v0

--- a/solution.py
+++ b/solution.py
@@ -8,6 +8,22 @@
 SUB = 32
 ITERS = 3
 step_length = 0.05
+
+
+def product_in_turn(value, axis, dim, product):
+    size, index, width = (lax.axis_size(axis), lax.axis_index(axis), value.shape[dim])
+    right = [(i, (i + 1) % size) for i in range(size)]
+    backward = [(i, (i - 1) % size) for i in range(size)]
+    middle = size // 2
+    from_left = from_right = value
+    total = product(value, index * width)
+    for lap in range(1, middle + 1):
+        from_left = lax.ppermute(from_left, axis, right)
+        if lap < size - middle:
+            from_right = lax.ppermute(from_right, axis, backward)
+            total = total + product(from_right, (index + lap) % size * width)
+        total = total + product(from_left, (index - lap) % size * width)
+    return total
 
 
 def exact_dot(left, right):
@@ -107,11 +123,16 @@
         local_shift = zero_shift
         for slot_pos in range(local_slices):
             local_shift = exact_dot(step_maps[slot_pos], local_shift) + offsets[slot_pos]
-        entry = lead_state + jnp.einsum(
-            "mij,mje->ie",
-            phi_rows,
-            lax.all_gather(local_shift[None], "tm", axis=0, tiled=True),
-            precision=lax.Precision.HIGHEST,
+        entry = lead_state + product_in_turn(
+            local_shift[None],
+            "tm",
+            0,
+            lambda shard, offset: jnp.einsum(
+                "mij,mje->ie",
+                lax.dynamic_slice_in_dim(phi_rows, offset, shard.shape[0], axis=0),
+                shard,
+                precision=lax.Precision.HIGHEST,
+            ),
         )
         start_list = []
         end_list = []

time: 318 us -> 300 us (0.943)
  blocking collectives: 187 us -> 56.5 us
  starting transfers between devices: 0 us -> 58.1 us
  waiting for transfers between devices: 0 us -> 47.4 us
  matrix products: 111 us -> 117 us
    all_gather x4 -> x0, blocking collectives: 126 us -> none  [sweep(): lax.all_gather(local_shift[None], 'tm', axis=0, tiled=True)]
    ppermute x0 -> x28, starting transfers between devices: none -> 58.1 us  [the longest x12 55.6 us: product_in_turn(): from_right = lax.ppermute(from_right, axis, backward)]
    ppermute x0 -> x28, waiting for transfers between devices: none -> 47.4 us  [the longest x16 47.3 us: product_in_turn(): from_left = lax.ppermute(from_left, axis, right)]
    dot_general x4 -> x32, matrix products: 2.69 us -> 8.62 us  [sweep(): jnp.einsum('mij,mje->ie', lax.dynamic_slice_in_dim(phi_rows, offset, shar...]
    pmax x1, blocking collectives: 21.2 us -> 17.1 us  [body(): records.append(lax.pmax(local_max, 'tm'))]
  transfers between devices with their start and end apart: 0 -> 28, of which waited for: 0 -> 15; matrix products, arithmetic and copies ran while one was open for 0% -> 5% of each run, Pallas kernels for 0% -> 0%
where the time goes in v1:
time: 300 us; the launch traced here: 299 us
  matrix products  117 us (39%)
  starting transfers between devices  58.1 us (19%)
  blocking collectives  56.5 us (19%)
  waiting for transfers between devices  47.4 us (16%)
  local copies, waits for them, and re-layouts  9.3 us (3%)
  loops' own time  7.21 us (2%)
    dot_general x220, matrix products, exact_dot(): jnp.dot(left, right, precision=lax.Precision.HIGHEST, preferred_element_t...  108 us
    ppermute x12, starting transfers between devices, product_in_turn(): from_right = lax.ppermute(from_right, axis, backward)  55.6 us
    ppermute x16, waiting for transfers between devices, product_in_turn(): from_left = lax.ppermute(from_left, axis, right)  47.3 us
    all_gather x1, blocking collectives, body(): all_maps = lax.all_gather(device_map[None], 'tm', axis=0, tiled=True)  31 us
    pmax x1, blocking collectives, body(): records.append(lax.pmax(local_max, 'tm'))  17.1 us
    dot_general x32, matrix products, sweep(): jnp.einsum('mij,mje->ie', lax.dynamic_slice_in_dim(phi_rows, offset, shar...  8.62 us
    psum x1, blocking collectives, body(): totals = lax.psum(jnp.sum(contact_float, axis=1), 'env')  8.4 us
  transfers between devices with their start and end apart: 28, of which 15 were waited for; matrix products, arithmetic and copies ran while one was open for 5% of the time, Pallas kernels for 0%

profile of v1, /device:TPU:0, one launch (start us, length us, event | category | flops | bytes accessed | tf_op | source)
XLA Modules:
  0.0 299.1 jit_solution(4891961708235912567)
XLA Ops:
  1.5 8.4 %psum.7 = f32[4]{0:T(128)S(1)} all-reduce(f32[4]{0:T(128)S(1)} %convert_reduce_fusion), channel_id=1, replica_groups=mesh['tm'=8,'env'=4] {'env'}, use_global_device_ids=true, to_apply=%region_1.0 | all-reduce | flops 4 | bytes 32 | tf_op jit(solution)/shard_map/psum | solution.py:90
  20.1 31.0 %all-gather.1 = f32[8,70,70]{2,1,0:T(8,128)S(1)} all-gather(f32[1,70,70]{2,1,0:T(8,128)S(1)} %convolution_bitcast_fusion.1), channel_id=2, replica_groups=mesh['tm'=8,'env'=4] {'tm'}, dimensions={0}, use_global_device_ids=true | all-gather | bytes 176400 | tf_op jit(solution)/shard_map/all_gather | solution.py:108
  51.1 12.9 %while.95 = (s32[]{:T(128)}, f32[70,70]{0,1:T(8,128)S(1)}, f32[8,70,70]{1,2,0:T(8,128)S(1)}, s32[8]{0:T(128)S(1)}, s32[]{:T(128)}, /*index=5*/f32[8,70,70]{2,1,0:T(8,128)S(1)}, s32[]{:T(128)}, s32[]{:T(128)}) while((s32[]{:T(128)}, f32[70,70]{0,1:T(8,128)S(1)}, f32[8,70,70]{1,2,0:T(8,128)S(1)}, s32[8]{0:T(128)S(1)}, s32[]{:T(128)}, ...), condition=%wide.region_3.4_spmd.clone, body=%wide.region_2.3_spmd.clone.sunk | while | flops 4135604 | bytes 206392 | solution.py:119
  72.3 4.8 %collective-permute-start.4 = (f32[1,70,256]{2,1,0:T(8,128)S(1)}, f32[1,70,256]{2,1,0:T(8,128)S(1)}, u32[]{:S(2)}, u32[]{:S(2)}) collective-permute-start(f32[1,70,256]{2,1,0:T(8,128)S(1)} %collective-permute-done.2), channel_id=1, source_target_pairs={{0,28},{4,0},{8,4},{12,8},{16,12},{20,16},{24,20},{28,24},{1,29},{... | collective-permute-start | bytes 215048 | tf_op jit(solution)/shard_map/ppermute | solution.py:23
  79.6 6.5 %collective-permute-done.6 = f32[1,70,256]{2,1,0:T(8,128)S(1)} collective-permute-done((f32[1,70,256]{2,1,0:T(8,128)S(1)}, f32[1,70,256]{2,1,0:T(8,128)S(1)}, u32[]{:S(2)}, u32[]{:S(2)}) %collective-permute-start.6) | collective-permute-done | bytes 71712 | tf_op jit(solution)/shard_map/ppermute | solution.py:21
  86.6 17.2 %while.89 = (s32[]{:T(128)}, f32[2,35,256]{2,1,0:T(8,128)S(1)}, f32[2,35,256]{2,1,0:T(8,128)S(1)}, f32[35]{0:T(128)S(1)}, f32[2,35,256]{2,1,0:T(8,128)S(1)}, /*i...) while((s32[]{:T(128)}, f32[2,35,256]{2,1,0:T(8,128)S(1)}, ...), condition=%wide.region_5.6_spmd, body=%wide.region_4.5_spmd.sunk | while | flops 62504960 | bytes 2680981 | solution.py:68
  103.8 17.2 %while.90 = (s32[]{:T(128)}, f32[2,35,256]{2,1,0:T(8,128)S(1)}, f32[2,35,256]{2,1,0:T(8,128)S(1)}, f32[35]{0:T(128)S(1)}, f32[2,35,256]{2,1,0:T(8,128)S(1)}, /*i...) while((s32[]{:T(128)}, f32[2,35,256]{2,1,0:T(8,128)S(1)}, ...), condition=%wide.region_7.8_spmd, body=%wide.region_6.7_spmd.sunk | while | flops 62504960 | bytes 2680981 | solution.py:68
  121.8 4.7 %collective-permute-start.7 = (f32[1,70,256]{2,1,0:T(8,128)S(1)}, f32[1,70,256]{2,1,0:T(8,128)S(1)}, u32[]{:S(2)}, u32[]{:S(2)}) collective-permute-start(f32[1,70,256]{2,1,0:T(8,128)S(1)} %bitcast.798), channel_id=1, source_target_pairs={{0,28},{4,0},{8,4},{12,8},{16,12},{20,16},{24,20},{28,24},{1,29},{... | collective-permute-start | bytes 215048 | tf_op jit(solution)/shard_map/ppermute | solution.py:23
  129.3 4.9 %collective-permute-start.9 = (f32[1,70,256]{2,1,0:T(8,128)S(1)}, f32[1,70,256]{2,1,0:T(8,128)S(1)}, u32[]{:S(2)}, u32[]{:S(2)}) collective-permute-start(f32[1,70,256]{2,1,0:T(8,128)S(1)} %collective-permute-done.7), channel_id=1, source_target_pairs={{0,28},{4,0},{8,4},{12,8},{16,12},{20,16},{24,20},{28,24},{1,29},{... | collective-permute-start | bytes 215048 | tf_op jit(solution)/shard_map/ppermute | solution.py:23
  136.7 4.8 %collective-permute-start.11 = (f32[1,70,256]{2,1,0:T(8,128)S(1)}, f32[1,70,256]{2,1,0:T(8,128)S(1)}, u32[]{:S(2)}, u32[]{:S(2)}) collective-permute-start(f32[1,70,256]{2,1,0:T(8,128)S(1)} %collective-permute-done.9), channel_id=1, source_target_pairs={{0,28},{4,0},{8,4},{12,8},{16,12},{20,16},{24,20},{28,24},{1,29},{... | collective-permute-start | bytes 215048 | tf_op jit(solution)/shard_map/ppermute | solution.py:23
  144.4 6.7 %collective-permute-done.13 = f32[1,70,256]{2,1,0:T(8,128)S(1)} collective-permute-done((f32[1,70,256]{2,1,0:T(8,128)S(1)}, f32[1,70,256]{2,1,0:T(8,128)S(1)}, u32[]{:S(2)}, u32[]{:S(2)}) %collective-permute-start.13) | collective-permute-done | bytes 71712 | tf_op jit(solution)/shard_map/ppermute | solution.py:21
  151.6 17.2 %while.91 = (s32[]{:T(128)}, f32[2,35,256]{2,1,0:T(8,128)S(1)}, f32[2,35,256]{2,1,0:T(8,128)S(1)}, f32[35]{0:T(128)S(1)}, f32[2,35,256]{2,1,0:T(8,128)S(1)}, /*i...) while((s32[]{:T(128)}, f32[2,35,256]{2,1,0:T(8,128)S(1)}, ...), condition=%wide.region_9.10_spmd, body=%wide.region_8.9_spmd.sunk | while | flops 62504960 | bytes 2680981 | solution.py:68
  168.8 17.2 %while.92 = (s32[]{:T(128)}, f32[2,35,256]{2,1,0:T(8,128)S(1)}, f32[2,35,256]{2,1,0:T(8,128)S(1)}, f32[35]{0:T(128)S(1)}, f32[2,35,256]{2,1,0:T(8,128)S(1)}, /*i...) while((s32[]{:T(128)}, f32[2,35,256]{2,1,0:T(8,128)S(1)}, ...), condition=%wide.region_11.12_spmd, body=%wide.region_10.11_spmd.sunk | while | flops 62504960 | bytes 2680981 | solution.py:68
  186.8 4.7 %collective-permute-start.14 = (f32[1,70,256]{2,1,0:T(8,128)S(1)}, f32[1,70,256]{2,1,0:T(8,128)S(1)}, u32[]{:S(2)}, u32[]{:S(2)}) collective-permute-start(f32[1,70,256]{2,1,0:T(8,128)S(1)} %bitcast.800), channel_id=1, source_target_pairs={{0,28},{4,0},{8,4},{12,8},{16,12},{20,16},{24,20},{28,24},{1,29},{... | collective-permute-start | bytes 215048 | tf_op jit(solution)/shard_map/ppermute | solution.py:23
  193.8 4.8 %collective-permute-start.16 = (f32[1,70,256]{2,1,0:T(8,128)S(1)}, f32[1,70,256]{2,1,0:T(8,128)S(1)}, u32[]{:S(2)}, u32[]{:S(2)}) collective-permute-start(f32[1,70,256]{2,1,0:T(8,128)S(1)} %collective-permute-done.14), channel_id=1, source_target_pairs={{0,28},{4,0},{8,4},{12,8},{16,12},{20,16},{24,20},{28,24},{1,29},{... | collective-permute-start | bytes 215048 | tf_op jit(solution)/shard_map/ppermute | solution.py:23
  201.2 4.8 %collective-permute-start.18 = (f32[1,70,256]{2,1,0:T(8,128)S(1)}, f32[1,70,256]{2,1,0:T(8,128)S(1)}, u32[]{:S(2)}, u32[]{:S(2)}) collective-permute-start(f32[1,70,256]{2,1,0:T(8,128)S(1)} %collective-permute-done.16), channel_id=1, source_target_pairs={{0,28},{4,0},{8,4},{12,8},{16,12},{20,16},{24,20},{28,24},{1,29},{... | collective-permute-start | bytes 215048 | tf_op jit(solution)/shard_map/ppermute | solution.py:23
  208.8 6.7 %collective-permute-done.20 = f32[1,70,256]{2,1,0:T(8,128)S(1)} collective-permute-done((f32[1,70,256]{2,1,0:T(8,128)S(1)}, f32[1,70,256]{2,1,0:T(8,128)S(1)}, u32[]{:S(2)}, u32[]{:S(2)}) %collective-permute-start.20) | collective-permute-done | bytes 71712 | tf_op jit(solution)/shard_map/ppermute | solution.py:21
  216.1 17.2 %while.93 = (s32[]{:T(128)}, f32[2,35,256]{2,1,0:T(8,128)S(1)}, f32[2,35,256]{2,1,0:T(8,128)S(1)}, f32[35]{0:T(128)S(1)}, f32[2,35,256]{2,1,0:T(8,128)S(1)}, /*i...) while((s32[]{:T(128)}, f32[2,35,256]{2,1,0:T(8,128)S(1)}, ...), condition=%wide.region_13.14_spmd, body=%wide.region_12.13_spmd.sunk | while | flops 62504960 | bytes 2680981 | solution.py:68
  233.3 17.1 %while.94 = (s32[]{:T(128)}, f32[2,35,256]{2,1,0:T(8,128)S(1)}, f32[2,35,256]{2,1,0:T(8,128)S(1)}, f32[35]{0:T(128)S(1)}, f32[2,35,256]{2,1,0:T(8,128)S(1)}, /*i...) while((s32[]{:T(128)}, f32[2,35,256]{2,1,0:T(8,128)S(1)}, ...), condition=%wide.region_15.16_spmd, body=%wide.region_14.15_spmd.sunk | while | flops 62504960 | bytes 2680981 | solution.py:68
  251.3 4.7 %collective-permute-start.21 = (f32[1,70,256]{2,1,0:T(8,128)S(1)}, f32[1,70,256]{2,1,0:T(8,128)S(1)}, u32[]{:S(2)}, u32[]{:S(2)}) collective-permute-start(f32[1,70,256]{2,1,0:T(8,128)S(1)} %bitcast.796), channel_id=1, source_target_pairs={{0,28},{4,0},{8,4},{12,8},{16,12},{20,16},{24,20},{28,24},{1,29},{... | collective-permute-start | bytes 215048 | tf_op jit(solution)/shard_map/ppermute | solution.py:23
  258.3 4.8 %collective-permute-start.23 = (f32[1,70,256]{2,1,0:T(8,128)S(1)}, f32[1,70,256]{2,1,0:T(8,128)S(1)}, u32[]{:S(2)}, u32[]{:S(2)}) collective-permute-start(f32[1,70,256]{2,1,0:T(8,128)S(1)} %collective-permute-done.21), channel_id=1, source_target_pairs={{0,28},{4,0},{8,4},{12,8},{16,12},{20,16},{24,20},{28,24},{1,29},{... | collective-permute-start | bytes 215048 | tf_op jit(solution)/shard_map/ppermute | solution.py:23
  265.7 4.8 %collective-permute-start.25 = (f32[1,70,256]{2,1,0:T(8,128)S(1)}, f32[1,70,256]{2,1,0:T(8,128)S(1)}, u32[]{:S(2)}, u32[]{:S(2)}) collective-permute-start(f32[1,70,256]{2,1,0:T(8,128)S(1)} %collective-permute-done.23), channel_id=1, source_target_pairs={{0,28},{4,0},{8,4},{12,8},{16,12},{20,16},{24,20},{28,24},{1,29},{... | collective-permute-start | bytes 215048 | tf_op jit(solution)/shard_map/ppermute | solution.py:23
  273.1 6.7 %collective-permute-done.27 = f32[1,70,256]{2,1,0:T(8,128)S(1)} collective-permute-done((f32[1,70,256]{2,1,0:T(8,128)S(1)}, f32[1,70,256]{2,1,0:T(8,128)S(1)}, u32[]{:S(2)}, u32[]{:S(2)}) %collective-permute-start.27) | collective-permute-done | bytes 71712 | tf_op jit(solution)/shard_map/ppermute | solution.py:21
  281.4 17.1 %all-reduce = (f32[1,256]{1,0:T(1,128)S(1)}, f32[1,256]{1,0:T(1,128)S(1)}, f32[1,256]{1,0:T(1,128)S(1)}) all-reduce(f32[1,256]{1,0:T(1,128)S(1)} %bitcast.803, f32[1,256]{1,0:T(1,128)S(1)} %bitcast.804, f32[1,256]{1,0:T(1,128)S(1)} %bitcast.802), channel_id=1, replica_groups=mesh['tm'=8,'env'=4] {'tm'}, use_global_device_ids=true, to_apply=%region_24.25 | all-reduce | flops 768 | bytes 6144 | tf_op jit(solution)/shard_map/pmax | solution.py:156
  (374 shorter events, 159.5 us)
Async XLA Ops:
  14.5 50.4 %collective-permute-start.1 = (f32[1,70,256]{2,1,0:T(8,128)S(1)}, f32[1,70,256]{2,1,0:T(8,128)S(1)}, u32[]{:S(2)}, u32[]{:S(2)}) collective-permute-start(f32[1,70,256]{2,1,0:T(8,128)S(1)} %bitcast.793), channel_id=1, source_target_pairs={{0,4},{4,8},{8,12},{12,16},{16,20},{20,24},{24,28},{28,0},{1,5},{5... | collective-permute-start | bytes 215048 | tf_op jit(solution)/shard_map/ppermute | solution.py:21
  16.0 48.9 %collective-permute-start = (f32[1,70,256]{2,1,0:T(8,128)S(1)}, f32[1,70,256]{2,1,0:T(8,128)S(1)}, u32[]{:S(2)}, u32[]{:S(2)}) collective-permute-start(f32[1,70,256]{2,1,0:T(8,128)S(1)} %bitcast.794), channel_id=1, source_target_pairs={{0,28},{4,0},{8,4},{12,8},{16,12},{20,16},{24,20},{28,24},{1,29},{... | collective-permute-start | bytes 215048 | tf_op jit(solution)/shard_map/ppermute | solution.py:23
  64.9 7.1 %collective-permute-start.3 = (f32[1,70,256]{2,1,0:T(8,128)S(1)}, f32[1,70,256]{2,1,0:T(8,128)S(1)}, u32[]{:S(2)}, u32[]{:S(2)}) collective-permute-start(f32[1,70,256]{2,1,0:T(8,128)S(1)} %collective-permute-done.1), channel_id=1, source_target_pairs={{0,4},{4,8},{8,12},{12,16},{16,20},{20,24},{24,28},{28,0},{1,5},{5... | collective-permute-start | bytes 215048 | tf_op jit(solution)/shard_map/ppermute | solution.py:21
  64.9 7.3 %collective-permute-start.2 = (f32[1,70,256]{2,1,0:T(8,128)S(1)}, f32[1,70,256]{2,1,0:T(8,128)S(1)}, u32[]{:S(2)}, u32[]{:S(2)}) collective-permute-start(f32[1,70,256]{2,1,0:T(8,128)S(1)} %collective-permute-done), channel_id=1, source_target_pairs={{0,28},{4,0},{8,4},{12,8},{16,12},{20,16},{24,20},{28,24},{1,29},{... | collective-permute-start | bytes 215048 | tf_op jit(solution)/shard_map/ppermute | solution.py:23
  72.0 7.0 %collective-permute-start.5 = (f32[1,70,256]{2,1,0:T(8,128)S(1)}, f32[1,70,256]{2,1,0:T(8,128)S(1)}, u32[]{:S(2)}, u32[]{:S(2)}) collective-permute-start(f32[1,70,256]{2,1,0:T(8,128)S(1)} %collective-permute-done.3), channel_id=1, source_target_pairs={{0,4},{4,8},{8,12},{12,16},{16,20},{20,24},{24,28},{28,0},{1,5},{5... | collective-permute-start | bytes 215048 | tf_op jit(solution)/shard_map/ppermute | solution.py:21
  79.0 7.1 %collective-permute-start.6 = (f32[1,70,256]{2,1,0:T(8,128)S(1)}, f32[1,70,256]{2,1,0:T(8,128)S(1)}, u32[]{:S(2)}, u32[]{:S(2)}) collective-permute-start(f32[1,70,256]{2,1,0:T(8,128)S(1)} %collective-permute-done.5), channel_id=1, source_target_pairs={{0,4},{4,8},{8,12},{12,16},{16,20},{20,24},{24,28},{28,0},{1,5},{5... | collective-permute-start | bytes 215048 | tf_op jit(solution)/shard_map/ppermute | solution.py:21
  121.7 7.6 %collective-permute-start.8 = (f32[1,70,256]{2,1,0:T(8,128)S(1)}, f32[1,70,256]{2,1,0:T(8,128)S(1)}, u32[]{:S(2)}, u32[]{:S(2)}) collective-permute-start(f32[1,70,256]{2,1,0:T(8,128)S(1)} %bitcast.797), channel_id=1, source_target_pairs={{0,4},{4,8},{8,12},{12,16},{16,20},{20,24},{24,28},{28,0},{1,5},{5... | collective-permute-start | bytes 215048 | tf_op jit(solution)/shard_map/ppermute | solution.py:21
  121.8 7.5 %collective-permute-start.7 = (f32[1,70,256]{2,1,0:T(8,128)S(1)}, f32[1,70,256]{2,1,0:T(8,128)S(1)}, u32[]{:S(2)}, u32[]{:S(2)}) collective-permute-start(f32[1,70,256]{2,1,0:T(8,128)S(1)} %bitcast.798), channel_id=1, source_target_pairs={{0,28},{4,0},{8,4},{12,8},{16,12},{20,16},{24,20},{28,24},{1,29},{... | collective-permute-start | bytes 215048 | tf_op jit(solution)/shard_map/ppermute | solution.py:23
  129.3 7.2 %collective-permute-start.10 = (f32[1,70,256]{2,1,0:T(8,128)S(1)}, f32[1,70,256]{2,1,0:T(8,128)S(1)}, u32[]{:S(2)}, u32[]{:S(2)}) collective-permute-start(f32[1,70,256]{2,1,0:T(8,128)S(1)} %collective-permute-done.8), channel_id=1, source_target_pairs={{0,4},{4,8},{8,12},{12,16},{16,20},{20,24},{24,28},{28,0},{1,5},{5... | collective-permute-start | bytes 215048 | tf_op jit(solution)/shard_map/ppermute | solution.py:21
  129.3 7.5 %collective-permute-start.9 = (f32[1,70,256]{2,1,0:T(8,128)S(1)}, f32[1,70,256]{2,1,0:T(8,128)S(1)}, u32[]{:S(2)}, u32[]{:S(2)}) collective-permute-start(f32[1,70,256]{2,1,0:T(8,128)S(1)} %collective-permute-done.7), channel_id=1, source_target_pairs={{0,28},{4,0},{8,4},{12,8},{16,12},{20,16},{24,20},{28,24},{1,29},{... | collective-permute-start | bytes 215048 | tf_op jit(solution)/shard_map/ppermute | solution.py:23
  136.5 7.0 %collective-permute-start.12 = (f32[1,70,256]{2,1,0:T(8,128)S(1)}, f32[1,70,256]{2,1,0:T(8,128)S(1)}, u32[]{:S(2)}, u32[]{:S(2)}) collective-permute-start(f32[1,70,256]{2,1,0:T(8,128)S(1)} %collective-permute-done.10), channel_id=1, source_target_pairs={{0,4},{4,8},{8,12},{12,16},{16,20},{20,24},{24,28},{28,0},{1,5},{5... | collective-permute-start | bytes 215048 | tf_op jit(solution)/shard_map/ppermute | solution.py:21
  136.7 7.3 %collective-permute-start.11 = (f32[1,70,256]{2,1,0:T(8,128)S(1)}, f32[1,70,256]{2,1,0:T(8,128)S(1)}, u32[]{:S(2)}, u32[]{:S(2)}) collective-permute-start(f32[1,70,256]{2,1,0:T(8,128)S(1)} %collective-permute-done.9), channel_id=1, source_target_pairs={{0,28},{4,0},{8,4},{12,8},{16,12},{20,16},{24,20},{28,24},{1,29},{... | collective-permute-start | bytes 215048 | tf_op jit(solution)/shard_map/ppermute | solution.py:23
  143.8 7.3 %collective-permute-start.13 = (f32[1,70,256]{2,1,0:T(8,128)S(1)}, f32[1,70,256]{2,1,0:T(8,128)S(1)}, u32[]{:S(2)}, u32[]{:S(2)}) collective-permute-start(f32[1,70,256]{2,1,0:T(8,128)S(1)} %collective-permute-done.12), channel_id=1, source_target_pairs={{0,4},{4,8},{8,12},{12,16},{16,20},{20,24},{24,28},{28,0},{1,5},{5... | collective-permute-start | bytes 215048 | tf_op jit(solution)/shard_map/ppermute | solution.py:21
  186.7 7.1 %collective-permute-start.15 = (f32[1,70,256]{2,1,0:T(8,128)S(1)}, f32[1,70,256]{2,1,0:T(8,128)S(1)}, u32[]{:S(2)}, u32[]{:S(2)}) collective-permute-start(f32[1,70,256]{2,1,0:T(8,128)S(1)} %bitcast.799), channel_id=1, source_target_pairs={{0,4},{4,8},{8,12},{12,16},{16,20},{20,24},{24,28},{28,0},{1,5},{5... | collective-permute-start | bytes 215048 | tf_op jit(solution)/shard_map/ppermute | solution.py:21
  193.8 7.0 %collective-permute-start.17 = (f32[1,70,256]{2,1,0:T(8,128)S(1)}, f32[1,70,256]{2,1,0:T(8,128)S(1)}, u32[]{:S(2)}, u32[]{:S(2)}) collective-permute-start(f32[1,70,256]{2,1,0:T(8,128)S(1)} %collective-permute-done.15), channel_id=1, source_target_pairs={{0,4},{4,8},{8,12},{12,16},{16,20},{20,24},{24,28},{28,0},{1,5},{5... | collective-permute-start | bytes 215048 | tf_op jit(solution)/shard_map/ppermute | solution.py:21
  193.8 7.3 %collective-permute-start.16 = (f32[1,70,256]{2,1,0:T(8,128)S(1)}, f32[1,70,256]{2,1,0:T(8,128)S(1)}, u32[]{:S(2)}, u32[]{:S(2)}) collective-permute-start(f32[1,70,256]{2,1,0:T(8,128)S(1)} %collective-permute-done.14), channel_id=1, source_target_pairs={{0,28},{4,0},{8,4},{12,8},{16,12},{20,16},{24,20},{28,24},{1,29},{... | collective-permute-start | bytes 215048 | tf_op jit(solution)/shard_map/ppermute | solution.py:23
  200.9 7.0 %collective-permute-start.19 = (f32[1,70,256]{2,1,0:T(8,128)S(1)}, f32[1,70,256]{2,1,0:T(8,128)S(1)}, u32[]{:S(2)}, u32[]{:S(2)}) collective-permute-start(f32[1,70,256]{2,1,0:T(8,128)S(1)} %collective-permute-done.17), channel_id=1, source_target_pairs={{0,4},{4,8},{8,12},{12,16},{16,20},{20,24},{24,28},{28,0},{1,5},{5... | collective-permute-start | bytes 215048 | tf_op jit(solution)/shard_map/ppermute | solution.py:21
  201.2 7.4 %collective-permute-start.18 = (f32[1,70,256]{2,1,0:T(8,128)S(1)}, f32[1,70,256]{2,1,0:T(8,128)S(1)}, u32[]{:S(2)}, u32[]{:S(2)}) collective-permute-start(f32[1,70,256]{2,1,0:T(8,128)S(1)} %collective-permute-done.16), channel_id=1, source_target_pairs={{0,28},{4,0},{8,4},{12,8},{16,12},{20,16},{24,20},{28,24},{1,29},{... | collective-permute-start | bytes 215048 | tf_op jit(solution)/shard_map/ppermute | solution.py:23
  208.2 7.4 %collective-permute-start.20 = (f32[1,70,256]{2,1,0:T(8,128)S(1)}, f32[1,70,256]{2,1,0:T(8,128)S(1)}, u32[]{:S(2)}, u32[]{:S(2)}) collective-permute-start(f32[1,70,256]{2,1,0:T(8,128)S(1)} %collective-permute-done.19), channel_id=1, source_target_pairs={{0,4},{4,8},{8,12},{12,16},{16,20},{20,24},{24,28},{28,0},{1,5},{5... | collective-permute-start | bytes 215048 | tf_op jit(solution)/shard_map/ppermute | solution.py:21
  251.2 7.1 %collective-permute-start.22 = (f32[1,70,256]{2,1,0:T(8,128)S(1)}, f32[1,70,256]{2,1,0:T(8,128)S(1)}, u32[]{:S(2)}, u32[]{:S(2)}) collective-permute-start(f32[1,70,256]{2,1,0:T(8,128)S(1)} %bitcast.795), channel_id=1, source_target_pairs={{0,4},{4,8},{8,12},{12,16},{16,20},{20,24},{24,28},{28,0},{1,5},{5... | collective-permute-start | bytes 215048 | tf_op jit(solution)/shard_map/ppermute | solution.py:21
  258.3 7.1 %collective-permute-start.24 = (f32[1,70,256]{2,1,0:T(8,128)S(1)}, f32[1,70,256]{2,1,0:T(8,128)S(1)}, u32[]{:S(2)}, u32[]{:S(2)}) collective-permute-start(f32[1,70,256]{2,1,0:T(8,128)S(1)} %collective-permute-done.22), channel_id=1, source_target_pairs={{0,4},{4,8},{8,12},{12,16},{16,20},{20,24},{24,28},{28,0},{1,5},{5... | collective-permute-start | bytes 215048 | tf_op jit(solution)/shard_map/ppermute | solution.py:21
  258.3 7.4 %collective-permute-start.23 = (f32[1,70,256]{2,1,0:T(8,128)S(1)}, f32[1,70,256]{2,1,0:T(8,128)S(1)}, u32[]{:S(2)}, u32[]{:S(2)}) collective-permute-start(f32[1,70,256]{2,1,0:T(8,128)S(1)} %collective-permute-done.21), channel_id=1, source_target_pairs={{0,28},{4,0},{8,4},{12,8},{16,12},{20,16},{24,20},{28,24},{1,29},{... | collective-permute-start | bytes 215048 | tf_op jit(solution)/shard_map/ppermute | solution.py:23
  265.7 7.1 %collective-permute-start.25 = (f32[1,70,256]{2,1,0:T(8,128)S(1)}, f32[1,70,256]{2,1,0:T(8,128)S(1)}, u32[]{:S(2)}, u32[]{:S(2)}) collective-permute-start(f32[1,70,256]{2,1,0:T(8,128)S(1)} %collective-permute-done.23), channel_id=1, source_target_pairs={{0,28},{4,0},{8,4},{12,8},{16,12},{20,16},{24,20},{28,24},{1,29},{... | collective-permute-start | bytes 215048 | tf_op jit(solution)/shard_map/ppermute | solution.py:23
  272.7 7.1 %collective-permute-start.27 = (f32[1,70,256]{2,1,0:T(8,128)S(1)}, f32[1,70,256]{2,1,0:T(8,128)S(1)}, u32[]{:S(2)}, u32[]{:S(2)}) collective-permute-start(f32[1,70,256]{2,1,0:T(8,128)S(1)} %collective-permute-done.26), channel_id=1, source_target_pairs={{0,4},{4,8},{8,12},{12,16},{16,20},{20,24},{24,28},{28,0},{1,5},{5... | collective-permute-start | bytes 215048 | tf_op jit(solution)/shard_map/ppermute | solution.py:21
  (13 other events, 98.0 us)
